TPU v7x, 768 devices: a whole 4x8x12 slice. The times are simulated.
768 devices in a mesh: grp: 32 (over y, x), wide: 24 (over z, core).
Axes of the slice: x: 4, y: 8, z: 12, core: 2. Of those that a mesh axis runs over, the one named last changes fastest.
Arguments:
- gradient: bfloat16 [32, 24, 96, 4096], P('grp', 'wide'), may hold values from -6 to 6
- residual: float32 [32, 24, 96, 4096], P('grp', 'wide'), may hold values from -4 to 4
- selected: int32 [32, 24, 24, 32], P('grp', 'wide'), may hold values from 0 to 127, as said below
- counts: int32 [32, 24, 24], P('grp', 'wide'), may hold values from 1 to 32, as said below
Outputs:
- update: float32 [24, 4, 4096], P('wide')
- new_residual: float32 [32, 24, 96, 4096], P('grp', 'wide')
Inputs may be any that keep to these rules, and one draw needn't show every extreme that they name: `selected`: for each device and shard, 32 distinct block numbers of that shard; entries at or past the count are ignored. `counts`: one shard has 32 on every device; every device has at most one other shard at 32, the rest at most 16.
All inputs are finite; a program needn't handle non-finite values.
Results may differ from a plain program's by a relative error of at most 0.0003.
Values sent between devices are 32-bit elements; how exact they have to be, the bound alone decides.
A program may use at most 32 MiB of HBM per device.

v0:
```python
import jax
import jax.numpy as jnp
from jax import lax
from jax.sharding import PartitionSpec as P


def copy_for_each(x, axis):
    copies = jnp.broadcast_to(x, (lax.axis_size(axis), *x.shape))
    return lax.all_to_all(copies, axis, split_axis=0, concat_axis=0, tiled=True)


def taken_together(x, axis):
    return copy_for_each(x, axis).sum(axis=0)


def body(gradient, residual, selected, counts):
    shards = lax.axis_size("wide")
    groups = lax.axis_size("grp")
    rows = gradient.shape[2]
    width = gradient.shape[3]
    block_len = 128
    own_rows = rows // shards
    own_blocks = own_rows * width // block_len
    slots = selected.shape[3]
    accumulated = gradient[0, 0].astype(jnp.float32) + residual[0, 0]
    blocks = accumulated.reshape(shards, own_blocks, block_len)
    picks = selected[0, 0]
    used = counts[0, 0]
    block_ids = jnp.arange(own_blocks, dtype=jnp.int32)
    one_hot = (picks[:, :, None] == block_ids).astype(jnp.float32)
    valid = (jnp.arange(slots, dtype=jnp.int32)[None, :] < used[:, None]).astype(jnp.float32)
    mask = jnp.einsum("wk,wkb->wb", valid, one_hot, precision=lax.Precision.HIGHEST)
    new_residual = (blocks * (1.0 - mask[..., None])).reshape(1, 1, rows, width)
    chosen = (
        jnp.einsum("wkb,wbc->wkc", one_hot, blocks, precision=lax.Precision.HIGHEST)
        * valid[..., None]
    )
    chosen_ids = picks.astype(jnp.float32)
    arrived, arrived_ids = (
        lax.all_to_all(chosen, "wide", split_axis=0, concat_axis=0, tiled=True),
        lax.all_to_all(chosen_ids, "wide", split_axis=0, concat_axis=0, tiled=True),
    )
    arrived_hot = (arrived_ids[:, :, None] == block_ids.astype(jnp.float32)).astype(jnp.float32)
    partial_sum = jnp.einsum("skb,skc->bc", arrived_hot, arrived, precision=lax.Precision.HIGHEST)
    summed = taken_together(partial_sum, "grp")
    update = (summed / groups).reshape(1, own_rows, width)
    return (update, new_residual)


def solution(mesh):
    return jax.shard_map(
        body,
        mesh=mesh,
        in_specs=(
            P("grp", "wide", None, None),
            P("grp", "wide", None, None),
            P("grp", "wide", None, None),
            P("grp", "wide", None),
        ),
        out_specs=(P("wide", None, None), P("grp", "wide", None, None)),
        check_vma=False,
    )
```

profile of v0, /device:TPU:6, one launch (start us, length us, event | category | flops | bytes accessed | tf_op | source)
XLA Modules:
  0.0 115.5 jit_solution(12745629505204364499)
XLA Ops:
  0.6 1.3 %convert_element_type.35 = f32[1,1,24,32]{3,2,1,0:T(8,128)} convert(s32[1,1,24,32]{3,2,1,0:T(8,128)} %param.6) | non-fusion elementwise | flops 768 | bytes 6144 | tf_op jit(solution)/shard_map/convert_element_type | solution.py:38
  1.9 15.4 %all-to-all-start = ((f32[24,1,32]{2,1,0:T(1,128)}), f32[24,1,32]{2,1,0:T(1,128)S(1)}, u32[]{:S(2)}, u32[]{:S(2)}) async-start(f32[24,1,32]{2,1,0:T(1,128)} %bitcast), calls=%async_computation | async-start | bytes 24576 | tf_op jit(solution)/shard_map/all_to_all | solution.py:41
  17.3 0.7 fusion.8
  18.0 1.0 fusion
  19.0 0.5 mul.21
  19.5 0.3 mul.22
  19.8 3.1 %fusion.9 = (f32[1,1,96,4096]{3,2,1,0:T(8,128)}, f32[1,1,96,4096]{3,2,1,0:T(8,128)S(1)}) fusion(f32[1,1,96,4096]{3,2,1,0:T(8,128)S(1)} %mul.22, f32[1,1,96,4096]{3,2,1,0:T(8,128)} %param.5, bf16[1,1,96,4096]{3,2,1,0:T(8,128)(2,1)} %param.4), kind=kLoop, calls=%fused_computation.17 | loop fusion | flops 1179648 | bytes 7077888 | tf_op jit(solution)/shard_map/mul | solution.py:33
  22.9 0.0 copy-start
  22.9 0.2 add.9
  23.1 0.5 copy-done
  23.6 1.6 %convolution_multiply_fusion = f32[24,32,128]{2,1,0:T(8,128)} fusion(f32[24,128,128]{2,1,0:T(8,128)S(1)} %add.9, f32[24,32]{1,0:T(8,128)S(1)} %get-tuple-element.4, s32[24,32]{1,0:T(8,128)S(1)} %bitcast.15), kind=kOutput, calls=%fused_computation.1 | convolution fusion | flops 151191552 | bytes 1972224 | tf_op jit(solution)/shard_map/wkb,wbc->wkc/dot_general | solution.py:35
  25.2 1.9 %all-to-all-done = f32[24,1,32]{2,1,0:T(1,128)S(1)} async-done(((f32[24,1,32]{2,1,0:T(1,128)}), f32[24,1,32]{2,1,0:T(1,128)S(1)}, u32[]{:S(2)}, u32[]{:S(2)}) %all-to-all-start) | async-done | bytes 3104 | tf_op jit(solution)/shard_map/all_to_all | solution.py:41
  27.2 7.8 %all-to-all-start.1 = ((f32[24,32,128]{2,1,0:T(8,128)}), f32[24,32,128]{2,1,0:T(8,128)S(1)}, u32[]{:S(2)}, u32[]{:S(2)}) async-start(f32[24,32,128]{2,1,0:T(8,128)} %convolution_multiply_fusion), calls=%async_computation.1 | async-start | bytes 786432 | tf_op jit(solution)/shard_map/all_to_all | solution.py:40
  34.9 20.7 %all-to-all-done.1 = f32[24,32,128]{2,1,0:T(8,128)S(1)} async-done(((f32[24,32,128]{2,1,0:T(8,128)}), f32[24,32,128]{2,1,0:T(8,128)S(1)}, u32[]{:S(2)}, u32[]{:S(2)}) %all-to-all-start.1) | async-done | bytes 393248 | tf_op jit(solution)/shard_map/all_to_all | solution.py:40
  55.6 0.6 convolution_bitcast_fusion
  56.2 0.2 broadcast_in_dim.2
  56.5 58.3 %all_to_all.16 = f32[32,128,128]{2,1,0:T(8,128)S(1)} all-to-all(f32[32,128,128]{2,1,0:T(8,128)S(1)} %broadcast_in_dim.2), channel_id=1, replica_groups=mesh['grp'=32,'wide'=24] {'grp'}, dimensions={0} | all-to-all | bytes 4194304 | tf_op jit(solution)/shard_map/all_to_all | solution.py:9
  114.7 0.1 reduce_sum.9
  114.9 0.7 div.10
  (3 shorter events, 0.0 us)
Async XLA Ops:
  1.9 25.2 %all-to-all-start = ((f32[24,1,32]{2,1,0:T(1,128)}), f32[24,1,32]{2,1,0:T(1,128)S(1)}, u32[]{:S(2)}, u32[]{:S(2)}) async-start(f32[24,1,32]{2,1,0:T(1,128)} %bitcast), calls=%async_computation | async-start | bytes 24576 | tf_op jit(solution)/shard_map/all_to_all | solution.py:41
  22.9 0.7 copy-start
  27.2 28.5 %all-to-all-start.1 = ((f32[24,32,128]{2,1,0:T(8,128)}), f32[24,32,128]{2,1,0:T(8,128)S(1)}, u32[]{:S(2)}, u32[]{:S(2)}) async-start(f32[24,32,128]{2,1,0:T(8,128)} %convolution_multiply_fusion), calls=%async_computation.1 | async-start | bytes 786432 | tf_op jit(solution)/shard_map/all_to_all | solution.py:40
where the time goes:
time: 116 us
  blocking collectives  58.3 us (50%)
  starting transfers between devices  23.1 us (20%)
  waiting for transfers between devices  22.6 us (19%)
  other arithmetic  5.25 us (5%)
  matrix products  3.21 us (3%)
  local copies, waits for them, and re-layouts  2.35 us (2%)
    all_to_all x1, blocking collectives, copy_for_each(): return lax.all_to_all(copies, axis, split_axis=0, concat_axis=0, tiled=True)  58.3 us
    all_to_all x1, waiting for transfers between devices, body(): lax.all_to_all(chosen, 'wide', split_axis=0, concat_axis=0, tiled=True)  20.7 us
    all_to_all x1, starting transfers between devices, body(): lax.all_to_all(chosen_ids, 'wide', split_axis=0, concat_axis=0, tiled=True)  15.4 us
    all_to_all x1, starting transfers between devices, body(): lax.all_to_all(chosen, 'wide', split_axis=0, concat_axis=0, tiled=True)  7.76 us
    mul x1, other arithmetic, body(): new_residual = (blocks * (1.0 - mask[..., None])).reshape(1, 1, rows, width)  3.08 us
  transfers between devices with their start and end apart: 2, of which 2 were waited for; matrix products, arithmetic and copies ran while one was open for 6% of the time, Pallas kernels for 0%

commit v1 on v0

v1 whole, which is shorter than its diff:
```python
import jax
import jax.numpy as jnp
from jax import lax
from jax.experimental import pallas as pl
from jax.experimental.pallas import tpu as pltpu
from jax.sharding import PartitionSpec as P

MESH = pl.DeviceIdType.MESH
NX, NY, NZ, NC = 4, 8, 12, 2
CHUNKS = 3
F32, BF16, I32 = jnp.float32, jnp.bfloat16, jnp.int32


def ring(d, n):
    return min(d % n, (-d) % n)


XC = sorted(
    [(dx, dc) for dx in range(NX) for dc in range(NC) if dx or dc],
    key=lambda o: -(2 * ring(o[0], NX) + o[1]),
)
YS = sorted(range(1, NY), key=lambda d: -ring(d, NY))
GS = sorted(
    [(dx, dy) for dx in range(NX) for dy in range(NY) if dx or dy],
    key=lambda o: -(ring(o[0], NX) + ring(o[1], NY)),
)


def halves(v):
    hi = v.astype(BF16)
    lo = (v - hi.astype(F32)).astype(BF16)
    return jnp.concatenate([hi, lo], axis=1)


def joined(v):
    return v[:, :128] + v[:, 128:]


def kernel(
    g_hbm, r_hbm, sel_ref, cnt_ref, upd_ref, nr_hbm,
    gv, rv, nrv, xsend, xrecv, idsend, idrecv, ysend, yrecv, zsend, zrecv, fin, gbuf,
    gsem, rsem, nsem, xs, xr, ids_s, ids_r, ys, yr, zs, zr, as_, ar,
):
    gi = lax.axis_index("grp")
    wi = lax.axis_index("wide")
    x, y = lax.rem(gi, NX), lax.div(gi, NX)
    z, c = lax.div(wi, NC), lax.rem(wi, NC)

    def dev(x_, y_, z_, c_):
        return (y_ * NX + x_, z_ * NC + c_)

    def mod(a, n):
        return lax.rem(a + n, n)

    loads = []
    for j in range(CHUNKS):
        rows = pl.ds(32 * j, 32)
        a = pltpu.make_async_copy(g_hbm.at[0, 0, rows], gv.at[rows], gsem.at[j])
        b = pltpu.make_async_copy(r_hbm.at[0, 0, rows], rv.at[rows], rsem.at[j])
        a.start()
        b.start()
        loads.append((a, b))

    barrier = pltpu.get_barrier_semaphore()
    zx = lax.rem(z, NX)
    for dz in sorted(range(1, NZ), key=lambda d: -ring(d, NZ)):
        pl.semaphore_signal(barrier, inc=1, device_id=dev(zx, y, mod(z + dz, NZ), c), device_id_type=MESH)
    for dx, dy in GS:
        pl.semaphore_signal(
            barrier, inc=1, device_id=dev(mod(x + dx, NX), mod(y + dy, NY), z, c), device_id_type=MESH
        )
    for dx in range(NX):
        pl.semaphore_signal(
            barrier, inc=1, device_id=dev(mod(x + dx, NX), y, z, mod(c + 1, NC)), device_id_type=MESH
        )

    sel = sel_ref[0, 0]
    eye = lax.broadcasted_iota(I32, (24, 24), 0) == lax.broadcasted_iota(I32, (24, 24), 1)
    used = jnp.sum(
        jnp.where(eye, jnp.broadcast_to(cnt_ref[0], (24, 24)).astype(F32), 0.0), axis=1, keepdims=True
    ).astype(I32)
    valid = lax.broadcasted_iota(I32, (24, 32), 1) < used
    low, high = jnp.bitwise_and(sel, 31), jnp.right_shift(sel, 5)
    target = jnp.where(valid, low * 4 + high, 512)
    odd = jnp.bitwise_and(lax.broadcasted_iota(I32, (24, 32), 0), 1)
    source = jnp.where(valid, low * 8 + high + 4 * odd, 512)
    target4 = jnp.concatenate([target] * 4, axis=1)
    source4 = jnp.concatenate([source] * 4, axis=1)
    for j in range(CHUNKS):
        for d in range(8):
            idsend[j, d] = target4[8 * j + d : 8 * j + d + 1]
    source_t = jnp.transpose(source4.astype(F32)).astype(I32)
    lane128 = lax.broadcasted_iota(I32, (1, 128), 1)
    lane256 = lax.broadcasted_iota(I32, (64, 256), 1)
    sub256 = lax.broadcasted_iota(I32, (256, 128), 0)
    ones = jnp.ones((128, 128), BF16)

    owner_class = jnp.bitwise_and(z - x, 3)
    same = lax.div(4 - owner_class, 4)
    pl.semaphore_wait(barrier, 47 - 4 * same)

    mine = 2 * x + c
    pending = []
    idcopies = []
    for n, (dx, dc) in enumerate(XC):
        tx, tc = mod(x + dx, NX), mod(c + dc, NC)
        cp = pltpu.make_async_remote_copy(
            src_ref=idsend.at[:, 2 * tx + tc], dst_ref=idrecv.at[n + 1],
            send_sem=ids_s.at[n], recv_sem=ids_r.at[n],
            device_id=dev(tx, y, z, tc), device_id_type=MESH,
        )
        cp.start()
        idcopies.append(cp)
    idrecv[0] = idsend[:, mine]

    xcopies = []
    writes = []
    for j in range(CHUNKS):
        loads[j][0].wait()
        loads[j][1].wait()
        for p in range(4):
            s = 8 * j + 2 * p
            top = 32 * j + 8 * p
            blocks = []
            for q in range(32):
                lanes = slice(128 * q, 128 * (q + 1))
                blocks.append(gv[top : top + 8, lanes].astype(F32) + rv[top : top + 8, lanes])
            data = jnp.concatenate(blocks, axis=0)
            ids = jnp.concatenate(
                [
                    jnp.broadcast_to(source_t[:32, s : s + 1], (32, 256)),
                    jnp.broadcast_to(source_t[:32, s + 1 : s + 2], (32, 256)),
                ],
                axis=0,
            )
            pick = jnp.where(ids == lane256, 1.0, 0.0).astype(BF16)
            got = joined(jnp.dot(pick, halves(data), preferred_element_type=F32))
            xsend[j, 2 * p] = got[:32]
            xsend[j, 2 * p + 1] = got[32:]
            row = jnp.where(lane128 < 32, source4[s : s + 1], source4[s + 1 : s + 2])
            hit = jnp.where(jnp.broadcast_to(row, (256, 128)) == sub256, 1.0, 0.0).astype(BF16)
            mask = jnp.dot(hit, ones, preferred_element_type=F32)
            kept = jnp.where(mask > 0.5, 0.0, data)
            for q in range(32):
                nrv[top : top + 8, 128 * q : 128 * (q + 1)] = kept[8 * q : 8 * q + 8]
        copies = []
        for n, (dx, dc) in enumerate(XC):
            tx, tc = mod(x + dx, NX), mod(c + dc, NC)
            cp = pltpu.make_async_remote_copy(
                src_ref=xsend.at[j, 2 * tx + tc], dst_ref=xrecv.at[j, n + 1],
                send_sem=xs.at[j, n], recv_sem=xr.at[j, n],
                device_id=dev(tx, y, z, tc), device_id_type=MESH,
            )
            cp.start()
            copies.append(cp)
        xrecv[j, 0] = xsend[j, mine]
        xcopies.append(copies)
        rows = pl.ds(32 * j, 32)
        w = pltpu.make_async_copy(nrv.at[rows], nr_hbm.at[0, 0, rows], nsem.at[j])
        w.start()
        writes.append(w)

    for cp in idcopies:
        cp.wait_recv()
    quarter = jnp.right_shift(lane128, 5)
    sub128 = lax.broadcasted_iota(I32, (128, 256), 0)
    ycopies = []
    for j in range(CHUNKS):
        for cp in xcopies[j]:
            cp.wait_recv()
        parts = []
        for h in range(2):
            row = idrecv[4 * h, j]
            for q in range(1, 4):
                row = jnp.where(quarter == q, idrecv[4 * h + q, j], row)
            parts.append(row)
        ids = jnp.broadcast_to(jnp.concatenate(parts, axis=1), (128, 256))
        put = jnp.where(ids == sub128, 1.0, 0.0).astype(BF16)
        arrived = xrecv[j].reshape(256, 128)
        ysend[j] = joined(jnp.dot(put, halves(arrived), preferred_element_type=F32)).reshape(8, 16, 128)
        copies = []
        for n, dy in enumerate(YS):
            ty = mod(y + dy, NY)
            cp = pltpu.make_async_remote_copy(
                src_ref=ysend.at[j, ty], dst_ref=yrecv.at[j, n],
                send_sem=ys.at[j, n], recv_sem=yr.at[j, n],
                device_id=dev(x, ty, z, c), device_id_type=MESH,
            )
            cp.start()
            copies.append(cp)
        ycopies.append(copies)

    zcopies = []
    for j in range(CHUNKS):
        for cp in ycopies[j]:
            cp.wait_recv()
        total = ysend[j, y]
        for n in range(NY - 1):
            total = total + yrecv[j, n]
        for q in range(4):
            zsend[j, q] = total[4 * q : 4 * q + 4]
        tz = 4 * j + x
        for dq in (2, 1, 3):
            tq = mod(x + dq, NX)
            cp = pltpu.make_async_remote_copy(
                src_ref=zsend.at[j, tq], dst_ref=zrecv.at[z],
                send_sem=zs.at[j, dq], recv_sem=zr.at[z],
                device_id=dev(tq, y, tz, c), device_id_type=MESH,
            )
            cp.start()
            zcopies.append(cp)

        def same_x(j=j, tz=tz):
            return pltpu.make_async_remote_copy(
                src_ref=zsend.at[j, x], dst_ref=zrecv.at[z],
                send_sem=zs.at[j, 0], recv_sem=zr.at[z],
                device_id=dev(x, y, tz, c), device_id_type=MESH,
            )

        @pl.when(tz != z)
        def _():
            same_x().start()

        @pl.when(tz == z)
        def _():
            zrecv[z] = zsend[j, x]

    for s in range(NZ):
        @pl.when(jnp.logical_or(zx != x, z != s))
        def _():
            pltpu.make_async_remote_copy(
                src_ref=zsend.at[0, 0], dst_ref=zrecv.at[s],
                send_sem=zs.at[0, 0], recv_sem=zr.at[s],
                device_id=dev(x, y, z, 1 - c), device_id_type=MESH,
            ).wait_recv()

    result = zrecv[0]
    for s in range(1, NZ):
        result = result + zrecv[s]
    result = result * (1.0 / 32.0)
    fin[...] = result
    gcopies = []
    for n, (dx, dy) in enumerate(GS):
        cp = pltpu.make_async_remote_copy(
            src_ref=fin, dst_ref=gbuf.at[gi],
            send_sem=as_.at[n], recv_sem=ar.at[gi],
            device_id=dev(mod(x + dx, NX), mod(y + dy, NY), z, c), device_id_type=MESH,
        )
        cp.start()
        gcopies.append(cp)
    gbuf[gi] = result

    for cp in idcopies:
        cp.wait_send()
    for copies in xcopies + ycopies:
        for cp in copies:
            cp.wait_send()
    for cp in zcopies:
        cp.wait_send()
    for j in range(CHUNKS):
        tz = 4 * j + x

        @pl.when(tz != z)
        def _():
            pltpu.make_async_remote_copy(
                src_ref=zsend.at[j, x], dst_ref=zrecv.at[z],
                send_sem=zs.at[j, 0], recv_sem=zr.at[z],
                device_id=dev(x, y, tz, c), device_id_type=MESH,
            ).wait_send()
    for w in writes:
        w.wait()
    for n, (dx, dy) in enumerate(GS):
        sg = mod(y - dy, NY) * NX + mod(x - dx, NX)
        pltpu.make_async_remote_copy(
            src_ref=fin, dst_ref=gbuf.at[sg],
            send_sem=as_.at[n], recv_sem=ar.at[sg],
            device_id=dev(mod(x + dx, NX), mod(y + dy, NY), z, c), device_id_type=MESH,
        ).wait_recv()
    for cp in gcopies:
        cp.wait_send()
    for p in range(32):
        upd_ref[0, :, 128 * p : 128 * (p + 1)] = gbuf[p]


def body(gradient, residual, selected, counts):
    dma = pltpu.SemaphoreType.DMA
    vmem = pl.BlockSpec(memory_space=pltpu.VMEM)
    anyspace = pl.BlockSpec(memory_space=pl.ANY)
    return pl.pallas_call(
        kernel,
        name="owner_sums",
        out_shape=(
            jax.ShapeDtypeStruct((1, 4, 4096), F32),
            jax.ShapeDtypeStruct((1, 1, 96, 4096), F32),
        ),
        in_specs=[anyspace, anyspace, vmem, vmem],
        out_specs=(vmem, anyspace),
        scratch_shapes=[
            pltpu.VMEM((96, 4096), BF16),
            pltpu.VMEM((96, 4096), F32),
            pltpu.VMEM((96, 4096), F32),
            pltpu.VMEM((CHUNKS, 8, 32, 128), F32),
            pltpu.VMEM((CHUNKS, 8, 32, 128), F32),
            pltpu.VMEM((CHUNKS, 8, 1, 128), I32),
            pltpu.VMEM((8, CHUNKS, 1, 128), I32),
            pltpu.VMEM((CHUNKS, 8, 16, 128), F32),
            pltpu.VMEM((CHUNKS, 7, 16, 128), F32),
            pltpu.VMEM((CHUNKS, 4, 4, 128), F32),
            pltpu.VMEM((NZ, 4, 128), F32),
            pltpu.VMEM((4, 128), F32),
            pltpu.VMEM((32, 4, 128), F32),
            dma((CHUNKS,)), dma((CHUNKS,)), dma((CHUNKS,)),
            dma((CHUNKS, 7)), dma((CHUNKS, 7)),
            dma((7,)), dma((7,)),
            dma((CHUNKS, 7)), dma((CHUNKS, 7)),
            dma((CHUNKS, 4)), dma((NZ,)),
            dma((31,)), dma((32,)),
        ],
        compiler_params=pltpu.CompilerParams(collective_id=0, has_side_effects=True),
    )(gradient, residual, selected, counts)


def solution(mesh):
    return jax.shard_map(
        body,
        mesh=mesh,
        in_specs=(
            P("grp", "wide", None, None),
            P("grp", "wide", None, None),
            P("grp", "wide", None, None),
            P("grp", "wide", None),
        ),
        out_specs=(P("wide", None, None), P("grp", "wide", None, None)),
        check_vma=False,
    )
```

time: 116 us -> 49.4 us (0.43)
  the two profiles are of different devices: /device:TPU:6 before, /device:TPU:8 now
where the time goes in v1:
time: 49.4 us; the launch traced here: 49.1 us
  Pallas kernels  44.4 us (90%)
  local copies, waits for them, and re-layouts  4.12 us (8%)
  between operations  0.64 us (1%)
    pallas_call x1, Pallas kernels, body(): pl.pallas_call(kernel, name='owner_sums', out_shape=(jax.ShapeDtypeStruct...  44.4 us
    unnamed x2, local copies, waits for them, and re-layouts  4.12 us

profile of v1, /device:TPU:8, one launch (start us, length us, event | category | flops | bytes accessed | tf_op | source)
XLA Modules:
  0.0 49.1 jit_solution(11755861879777907893)
XLA Ops:
  0.6 44.4 %owner_sums.1 = (f32[1,4,4096]{2,1,0:T(4,128)}, f32[1,1,96,4096]{3,2,1,0:T(8,128)}) custom-call(bf16[1,1,96,4096]{3,2,1,0:T(8,128)(2,1)} %g_hbm.1, f32[1,1,96,4096]{3,2,1,0:T(8,128)} %r_hbm.1, s32[1,1,24,32]{3,2,1,0:T(8,128)} %sel_ref.1, s32[1,1,24]{2,1,0:T(1,128)} %cnt_ref.1), custom_call_target="tpu_custom_call" | custom-call | tf_op jit(solution)/shard_map/owner_sums/pallas_call | solution.py:289
  45.0 1.5 %copy.8 = f32[1,4,4096]{2,1,0:T(4,128)} copy(f32[1,4,4096]{2,1,0:T(4,128)} %get-tuple-element.4) | data formatting | bytes 131072
  46.5 2.7 %copy.9 = f32[1,1,96,4096]{3,2,1,0:T(8,128)} copy(f32[1,1,96,4096]{3,2,1,0:T(8,128)} %get-tuple-element.5) | data formatting | bytes 3145728

commit v2 on v1

--- a/solution.py
+++ b/solution.py
@@ -37,9 +37,9 @@
 
 
 def kernel(
-    g_hbm, r_hbm, sel_ref, cnt_ref, upd_ref, nr_hbm,
-    gv, rv, nrv, xsend, xrecv, idsend, idrecv, ysend, yrecv, zsend, zrecv, fin, gbuf,
-    gsem, rsem, nsem, xs, xr, ids_s, ids_r, ys, yr, zs, zr, as_, ar,
+    g_hbm, r_hbm, sel_hbm, cnt_hbm, upd_ref, nr_ref,
+    sel_ref, cnt_ref, gv, rv, xsend, xrecv, idsend, idrecv, ysend, yrecv, zsend, zrecv, fin, gbuf,
+    psem, gsem, rsem, xs, xr, ids_s, ids_r, ys, yr, zs, zr, as_, ar, near1, near2, near3,
 ):
     gi = lax.axis_index("grp")
     wi = lax.axis_index("wide")
@@ -52,6 +52,12 @@
     def mod(a, n):
         return lax.rem(a + n, n)
 
+    picks = (
+        pltpu.make_async_copy(sel_hbm, sel_ref, psem.at[0]),
+        pltpu.make_async_copy(cnt_hbm, cnt_ref, psem.at[1]),
+    )
+    for cp in picks:
+        cp.start()
     loads = []
     for j in range(CHUNKS):
         rows = pl.ds(32 * j, 32)
@@ -61,19 +67,19 @@
         b.start()
         loads.append((a, b))
 
+    def signal(sem, x_, y_, z_, c_):
+        pl.semaphore_signal(sem, inc=1, device_id=dev(x_, y_, z_, c_), device_id_type=MESH)
+
     barrier = pltpu.get_barrier_semaphore()
-    zx = lax.rem(z, NX)
-    for dz in sorted(range(1, NZ), key=lambda d: -ring(d, NZ)):
-        pl.semaphore_signal(barrier, inc=1, device_id=dev(zx, y, mod(z + dz, NZ), c), device_id_type=MESH)
-    for dx, dy in GS:
-        pl.semaphore_signal(
-            barrier, inc=1, device_id=dev(mod(x + dx, NX), mod(y + dy, NY), z, c), device_id_type=MESH
-        )
-    for dx in range(NX):
-        pl.semaphore_signal(
-            barrier, inc=1, device_id=dev(mod(x + dx, NX), y, z, mod(c + 1, NC)), device_id_type=MESH
-        )
-
+    for d in (1, NZ - 1):
+        signal(barrier, x, y, mod(z + d, NZ), c)
+    for d in (1, NY - 1):
+        signal(barrier, x, mod(y + d, NY), z, c)
+    for dx, dc in XC:
+        signal(barrier, mod(x + dx, NX), y, z, mod(c + dc, NC))
+
+    for cp in picks:
+        cp.wait()
     sel = sel_ref[0, 0]
     eye = lax.broadcasted_iota(I32, (24, 24), 0) == lax.broadcasted_iota(I32, (24, 24), 1)
     used = jnp.sum(
@@ -95,26 +101,9 @@
     sub256 = lax.broadcasted_iota(I32, (256, 128), 0)
     ones = jnp.ones((128, 128), BF16)
 
-    owner_class = jnp.bitwise_and(z - x, 3)
-    same = lax.div(4 - owner_class, 4)
-    pl.semaphore_wait(barrier, 47 - 4 * same)
-
     mine = 2 * x + c
-    pending = []
     idcopies = []
-    for n, (dx, dc) in enumerate(XC):
-        tx, tc = mod(x + dx, NX), mod(c + dc, NC)
-        cp = pltpu.make_async_remote_copy(
-            src_ref=idsend.at[:, 2 * tx + tc], dst_ref=idrecv.at[n + 1],
-            send_sem=ids_s.at[n], recv_sem=ids_r.at[n],
-            device_id=dev(tx, y, z, tc), device_id_type=MESH,
-        )
-        cp.start()
-        idcopies.append(cp)
-    idrecv[0] = idsend[:, mine]
-
     xcopies = []
-    writes = []
     for j in range(CHUNKS):
         loads[j][0].wait()
         loads[j][1].wait()
@@ -142,7 +131,29 @@
             mask = jnp.dot(hit, ones, preferred_element_type=F32)
             kept = jnp.where(mask > 0.5, 0.0, data)
             for q in range(32):
-                nrv[top : top + 8, 128 * q : 128 * (q + 1)] = kept[8 * q : 8 * q + 8]
+                nr_ref[0, 0, top : top + 8, 128 * q : 128 * (q + 1)] = kept[8 * q : 8 * q + 8]
+        if j == 0:
+            pl.semaphore_wait(barrier, 11)
+            for d in (1, NZ - 1):
+                signal(near1, x, y, mod(z + d, NZ), c)
+            for d in (1, NY - 1):
+                signal(near1, x, mod(y + d, NY), z, c)
+            for n, (dx, dc) in enumerate(XC):
+                tx, tc = mod(x + dx, NX), mod(c + dc, NC)
+                cp = pltpu.make_async_remote_copy(
+                    src_ref=idsend.at[:, 2 * tx + tc], dst_ref=idrecv.at[n + 1],
+                    send_sem=ids_s.at[n], recv_sem=ids_r.at[n],
+                    device_id=dev(tx, y, z, tc), device_id_type=MESH,
+                )
+                cp.start()
+                idcopies.append(cp)
+            idrecv[0] = idsend[:, mine]
+        if j == 1:
+            pl.semaphore_wait(near1, 4)
+            for d in (2, NZ - 2):
+                signal(near2, x, y, mod(z + d, NZ), c)
+            for d in (2, NY - 2):
+                signal(near2, x, mod(y + d, NY), z, c)
         copies = []
         for n, (dx, dc) in enumerate(XC):
             tx, tc = mod(x + dx, NX), mod(c + dc, NC)
@@ -155,11 +166,10 @@
             copies.append(cp)
         xrecv[j, 0] = xsend[j, mine]
         xcopies.append(copies)
-        rows = pl.ds(32 * j, 32)
-        w = pltpu.make_async_copy(nrv.at[rows], nr_hbm.at[0, 0, rows], nsem.at[j])
-        w.start()
-        writes.append(w)
-
+
+    pl.semaphore_wait(near2, 4)
+    for d in (3, NZ - 3):
+        signal(near3, x, y, mod(z + d, NZ), c)
     for cp in idcopies:
         cp.wait_recv()
     quarter = jnp.right_shift(lane128, 5)
@@ -190,6 +200,8 @@
             copies.append(cp)
         ycopies.append(copies)
 
+    pl.semaphore_wait(near3, 2)
+    zx = lax.rem(z, NX)
     zcopies = []
     for j in range(CHUNKS):
         for cp in ycopies[j]:
@@ -267,8 +279,6 @@
                 send_sem=zs.at[j, 0], recv_sem=zr.at[z],
                 device_id=dev(x, y, tz, c), device_id_type=MESH,
             ).wait_send()
-    for w in writes:
-        w.wait()
     for n, (dx, dy) in enumerate(GS):
         sg = mod(y - dy, NY) * NX + mod(x - dx, NX)
         pltpu.make_async_remote_copy(
@@ -282,22 +292,35 @@
         upd_ref[0, :, 128 * p : 128 * (p + 1)] = gbuf[p]
 
 
+def flush(upd_ref, nr_ref, upd_hbm, nr_hbm, sem):
+    copies = [pltpu.make_async_copy(upd_ref, upd_hbm, sem.at[4])]
+    for n in range(4):
+        rows = pl.ds(24 * n, 24)
+        copies.append(pltpu.make_async_copy(nr_ref.at[0, 0, rows], nr_hbm.at[0, 0, rows], sem.at[n]))
+    for cp in copies:
+        cp.start()
+    for cp in copies:
+        cp.wait()
+
+
 def body(gradient, residual, selected, counts):
     dma = pltpu.SemaphoreType.DMA
+    plain = pltpu.SemaphoreType.REGULAR
     vmem = pl.BlockSpec(memory_space=pltpu.VMEM)
-    anyspace = pl.BlockSpec(memory_space=pl.ANY)
-    return pl.pallas_call(
+    hbm = pl.BlockSpec(memory_space=pltpu.HBM)
+    update, rest = pl.pallas_call(
         kernel,
         name="owner_sums",
         out_shape=(
-            jax.ShapeDtypeStruct((1, 4, 4096), F32),
-            jax.ShapeDtypeStruct((1, 1, 96, 4096), F32),
+            pltpu.VMEM((1, 4, 4096), F32),
+            pltpu.VMEM((1, 1, 96, 4096), F32),
         ),
-        in_specs=[anyspace, anyspace, vmem, vmem],
-        out_specs=(vmem, anyspace),
+        in_specs=[hbm, hbm, hbm, hbm],
+        out_specs=(vmem, vmem),
         scratch_shapes=[
+            pltpu.VMEM((1, 1, 24, 32), I32),
+            pltpu.VMEM((1, 1, 24), I32),
             pltpu.VMEM((96, 4096), BF16),
-            pltpu.VMEM((96, 4096), F32),
             pltpu.VMEM((96, 4096), F32),
             pltpu.VMEM((CHUNKS, 8, 32, 128), F32),
             pltpu.VMEM((CHUNKS, 8, 32, 128), F32),
@@ -309,15 +332,28 @@
             pltpu.VMEM((NZ, 4, 128), F32),
             pltpu.VMEM((4, 128), F32),
             pltpu.VMEM((32, 4, 128), F32),
-            dma((CHUNKS,)), dma((CHUNKS,)), dma((CHUNKS,)),
+            dma((2,)), dma((CHUNKS,)), dma((CHUNKS,)),
             dma((CHUNKS, 7)), dma((CHUNKS, 7)),
             dma((7,)), dma((7,)),
             dma((CHUNKS, 7)), dma((CHUNKS, 7)),
             dma((CHUNKS, 4)), dma((NZ,)),
             dma((31,)), dma((32,)),
+            plain, plain, plain,
         ],
-        compiler_params=pltpu.CompilerParams(collective_id=0, has_side_effects=True),
+        compiler_params=pltpu.CompilerParams(collective_id=0, has_side_effects=True, vmem_limit_bytes=62 << 20),
     )(gradient, residual, selected, counts)
+    return pl.pallas_call(
+        flush,
+        name="write_results",
+        out_shape=(
+            jax.ShapeDtypeStruct((1, 4, 4096), F32),
+            jax.ShapeDtypeStruct((1, 1, 96, 4096), F32),
+        ),
+        in_specs=[vmem, vmem],
+        out_specs=(hbm, hbm),
+        scratch_shapes=[dma((5,))],
+        compiler_params=pltpu.CompilerParams(vmem_limit_bytes=1 << 20),
+    )(update, rest)
 
 
 def solution(mesh):

time: 49.4 us -> 41.3 us (0.84)
  local copies, waits for them, and re-layouts: 4.12 us -> 0 us
  Pallas kernels: 44.4 us -> 40.5 us
    unnamed x2 -> x0, local copies, waits for them, and re-layouts: 4.12 us -> none
    pallas_call x1 -> x2, Pallas kernels: 44.4 us -> 40.5 us  [the longest x1 39.3 us: body(): pl.pallas_call(kernel, name='owner_sums', out_shape=(pltpu.VMEM((1, 4, 40...]
where the time goes in v2:
time: 41.3 us; the launch traced here: 41.1 us
  Pallas kernels  40.5 us (98%)
  between operations  0.64 us (2%)
    pallas_call x1, Pallas kernels, body(): pl.pallas_call(kernel, name='owner_sums', out_shape=(pltpu.VMEM((1, 4, 40...  39.3 us
    pallas_call x1, Pallas kernels, body(): pl.pallas_call(flush, name='write_results', out_shape=(jax.ShapeDtypeStru...  1.2 us

profile of v2, /device:TPU:8, one launch (start us, length us, event | category | flops | bytes accessed | tf_op | source)
XLA Modules:
  0.0 41.1 jit_solution(17035452068793188727)
XLA Ops:
  0.6 39.3 %owner_sums.1 = (f32[1,4,4096]{2,1,0:T(4,128)S(1)}, f32[1,1,96,4096]{3,2,1,0:T(8,128)S(1)}) custom-call(bf16[1,1,96,4096]{3,2,1,0:T(8,128)(2,1)} %g_hbm.1, f32[1,1,96,4096]{3,2,1,0:T(8,128)} %r_hbm.1, s32[1,1,24,32]{3,2,1,0:T(8,128)} %sel_hbm.1, s32[1,1,24]{2,1,0:T(1,128)} %cnt_hbm.1), custom_call_target="tpu_custom_call" | custom-call | tf_op jit(solution)/shard_map/owner_sums/pallas_call | solution.py:311
  39.9 1.2 %write_results.1 = (f32[1,4,4096]{2,1,0:T(4,128)}, f32[1,1,96,4096]{3,2,1,0:T(8,128)}) custom-call(f32[1,4,4096]{2,1,0:T(4,128)S(1)} %get-tuple-element.4.upd_ref, f32[1,1,96,4096]{3,2,1,0:T(8,128)S(1)} %get-tuple-element.5.nr_ref), custom_call_target="tpu_custom_call" | custom-call | tf_op jit(solution)/shard_map/write_results/pallas_call | solution.py:345

commit v3 on v2

--- a/solution.py
+++ b/solution.py
@@ -202,30 +202,19 @@
 
     pl.semaphore_wait(near3, 2)
     zx = lax.rem(z, NX)
-    zcopies = []
     for j in range(CHUNKS):
         for cp in ycopies[j]:
             cp.wait_recv()
         total = ysend[j, y]
         for n in range(NY - 1):
             total = total + yrecv[j, n]
-        for q in range(4):
-            zsend[j, q] = total[4 * q : 4 * q + 4]
+        zsend[j] = total
         tz = 4 * j + x
-        for dq in (2, 1, 3):
-            tq = mod(x + dq, NX)
-            cp = pltpu.make_async_remote_copy(
-                src_ref=zsend.at[j, tq], dst_ref=zrecv.at[z],
-                send_sem=zs.at[j, dq], recv_sem=zr.at[z],
-                device_id=dev(tq, y, tz, c), device_id_type=MESH,
-            )
-            cp.start()
-            zcopies.append(cp)
 
         def same_x(j=j, tz=tz):
             return pltpu.make_async_remote_copy(
-                src_ref=zsend.at[j, x], dst_ref=zrecv.at[z],
-                send_sem=zs.at[j, 0], recv_sem=zr.at[z],
+                src_ref=zsend.at[j], dst_ref=zrecv.at[z],
+                send_sem=zs.at[j], recv_sem=zr.at[z],
                 device_id=dev(x, y, tz, c), device_id_type=MESH,
             )
 
@@ -235,61 +224,69 @@
 
         @pl.when(tz == z)
         def _():
-            zrecv[z] = zsend[j, x]
-
-    for s in range(NZ):
-        @pl.when(jnp.logical_or(zx != x, z != s))
-        def _():
+            zrecv[z] = zsend[j]
+
+    owner = zx == x
+
+    @pl.when(owner)
+    def _():
+        for s in range(NZ):
+            @pl.when(z != s)
+            def _():
+                pltpu.make_async_remote_copy(
+                    src_ref=zsend.at[0], dst_ref=zrecv.at[s],
+                    send_sem=zs.at[0], recv_sem=zr.at[s],
+                    device_id=dev(x, y, z, 1 - c), device_id_type=MESH,
+                ).wait_recv()
+
+        result = zrecv[0]
+        for s in range(1, NZ):
+            result = result + zrecv[s]
+        result = result * (1.0 / 32.0)
+        fin[...] = result
+        for n, (dx, dy) in enumerate(GS):
             pltpu.make_async_remote_copy(
-                src_ref=zsend.at[0, 0], dst_ref=zrecv.at[s],
-                send_sem=zs.at[0, 0], recv_sem=zr.at[s],
-                device_id=dev(x, y, z, 1 - c), device_id_type=MESH,
-            ).wait_recv()
-
-    result = zrecv[0]
-    for s in range(1, NZ):
-        result = result + zrecv[s]
-    result = result * (1.0 / 32.0)
-    fin[...] = result
-    gcopies = []
-    for n, (dx, dy) in enumerate(GS):
-        cp = pltpu.make_async_remote_copy(
-            src_ref=fin, dst_ref=gbuf.at[gi],
-            send_sem=as_.at[n], recv_sem=ar.at[gi],
-            device_id=dev(mod(x + dx, NX), mod(y + dy, NY), z, c), device_id_type=MESH,
-        )
-        cp.start()
-        gcopies.append(cp)
-    gbuf[gi] = result
+                src_ref=fin, dst_ref=gbuf.at[y],
+                send_sem=as_.at[n], recv_sem=ar.at[y],
+                device_id=dev(mod(x + dx, NX), mod(y + dy, NY), z, c), device_id_type=MESH,
+            ).start()
+        gbuf[y] = result
 
     for cp in idcopies:
         cp.wait_send()
     for copies in xcopies + ycopies:
         for cp in copies:
             cp.wait_send()
-    for cp in zcopies:
-        cp.wait_send()
     for j in range(CHUNKS):
         tz = 4 * j + x
 
         @pl.when(tz != z)
         def _():
             pltpu.make_async_remote_copy(
-                src_ref=zsend.at[j, x], dst_ref=zrecv.at[z],
-                send_sem=zs.at[j, 0], recv_sem=zr.at[z],
+                src_ref=zsend.at[j], dst_ref=zrecv.at[z],
+                send_sem=zs.at[j], recv_sem=zr.at[z],
                 device_id=dev(x, y, tz, c), device_id_type=MESH,
             ).wait_send()
-    for n, (dx, dy) in enumerate(GS):
-        sg = mod(y - dy, NY) * NX + mod(x - dx, NX)
-        pltpu.make_async_remote_copy(
-            src_ref=fin, dst_ref=gbuf.at[sg],
-            send_sem=as_.at[n], recv_sem=ar.at[sg],
-            device_id=dev(mod(x + dx, NX), mod(y + dy, NY), z, c), device_id_type=MESH,
-        ).wait_recv()
-    for cp in gcopies:
-        cp.wait_send()
+    for s in range(NY):
+        @pl.when(jnp.logical_or(zx != x, y != s))
+        def _():
+            pltpu.make_async_remote_copy(
+                src_ref=fin, dst_ref=gbuf.at[s],
+                send_sem=as_.at[0], recv_sem=ar.at[s],
+                device_id=dev(x, y, z, 1 - c), device_id_type=MESH,
+            ).wait_recv()
+
+    @pl.when(owner)
+    def _():
+        for n, (dx, dy) in enumerate(GS):
+            pltpu.make_async_remote_copy(
+                src_ref=fin, dst_ref=gbuf.at[y],
+                send_sem=as_.at[n], recv_sem=ar.at[y],
+                device_id=dev(mod(x + dx, NX), mod(y + dy, NY), z, c), device_id_type=MESH,
+            ).wait_send()
+
     for p in range(32):
-        upd_ref[0, :, 128 * p : 128 * (p + 1)] = gbuf[p]
+        upd_ref[0, :, 128 * p : 128 * (p + 1)] = gbuf[p // 4, 4 * (p % 4) : 4 * (p % 4) + 4]
 
 
 def flush(upd_ref, nr_ref, upd_hbm, nr_hbm, sem):
@@ -328,16 +325,16 @@
             pltpu.VMEM((8, CHUNKS, 1, 128), I32),
             pltpu.VMEM((CHUNKS, 8, 16, 128), F32),
             pltpu.VMEM((CHUNKS, 7, 16, 128), F32),
-            pltpu.VMEM((CHUNKS, 4, 4, 128), F32),
-            pltpu.VMEM((NZ, 4, 128), F32),
-            pltpu.VMEM((4, 128), F32),
-            pltpu.VMEM((32, 4, 128), F32),
+            pltpu.VMEM((CHUNKS, 16, 128), F32),
+            pltpu.VMEM((NZ, 16, 128), F32),
+            pltpu.VMEM((16, 128), F32),
+            pltpu.VMEM((NY, 16, 128), F32),
             dma((2,)), dma((CHUNKS,)), dma((CHUNKS,)),
             dma((CHUNKS, 7)), dma((CHUNKS, 7)),
             dma((7,)), dma((7,)),
             dma((CHUNKS, 7)), dma((CHUNKS, 7)),
-            dma((CHUNKS, 4)), dma((NZ,)),
-            dma((31,)), dma((32,)),
+            dma((CHUNKS,)), dma((NZ,)),
+            dma((31,)), dma((NY,)),
             plain, plain, plain,
         ],
         compiler_params=pltpu.CompilerParams(collective_id=0, has_side_effects=True, vmem_limit_bytes=62 << 20),

time: 41.3 us -> 40.5 us (0.981)
  the two profiles are of different devices: /device:TPU:8 before, /device:TPU:6 now
where the time goes in v3:
time: 40.5 us; the launch traced here: 40.3 us
  Pallas kernels  39.7 us (98%)
  between operations  0.64 us (2%)
    pallas_call x1, Pallas kernels, body(): pl.pallas_call(kernel, name='owner_sums', out_shape=(pltpu.VMEM((1, 4, 40...  38.5 us
    pallas_call x1, Pallas kernels, body(): pl.pallas_call(flush, name='write_results', out_shape=(jax.ShapeDtypeStru...  1.2 us

profile of v3, /device:TPU:6, one launch (start us, length us, event | category | flops | bytes accessed | tf_op | source)
XLA Modules:
  0.0 40.3 jit_solution(11106771766302932714)
XLA Ops:
  0.6 38.5 %owner_sums.1 = (f32[1,4,4096]{2,1,0:T(4,128)S(1)}, f32[1,1,96,4096]{3,2,1,0:T(8,128)S(1)}) custom-call(bf16[1,1,96,4096]{3,2,1,0:T(8,128)(2,1)} %g_hbm.1, f32[1,1,96,4096]{3,2,1,0:T(8,128)} %r_hbm.1, s32[1,1,24,32]{3,2,1,0:T(8,128)} %sel_hbm.1, s32[1,1,24]{2,1,0:T(1,128)} %cnt_hbm.1), custom_call_target="tpu_custom_call" | custom-call | tf_op jit(solution)/shard_map/owner_sums/pallas_call | solution.py:308
  39.1 1.2 %write_results.1 = (f32[1,4,4096]{2,1,0:T(4,128)}, f32[1,1,96,4096]{3,2,1,0:T(8,128)}) custom-call(f32[1,4,4096]{2,1,0:T(4,128)S(1)} %get-tuple-element.4.upd_ref, f32[1,1,96,4096]{3,2,1,0:T(8,128)S(1)} %get-tuple-element.5.nr_ref), custom_call_target="tpu_custom_call" | custom-call | tf_op jit(solution)/shard_map/write_results/pallas_call | solution.py:342

commit v4 on v3

--- a/solution.py
+++ b/solution.py
@@ -52,6 +52,17 @@
     def mod(a, n):
         return lax.rem(a + n, n)
 
+    def signal(sem, x_, y_, z_, c_):
+        pl.semaphore_signal(sem, inc=1, device_id=dev(x_, y_, z_, c_), device_id_type=MESH)
+
+    barrier = pltpu.get_barrier_semaphore()
+    for d in (1, NZ - 1):
+        signal(barrier, x, y, mod(z + d, NZ), c)
+    for d in (1, NY - 1):
+        signal(barrier, x, mod(y + d, NY), z, c)
+    for dx, dc in XC:
+        signal(barrier, mod(x + dx, NX), y, z, mod(c + dc, NC))
+
     picks = (
         pltpu.make_async_copy(sel_hbm, sel_ref, psem.at[0]),
         pltpu.make_async_copy(cnt_hbm, cnt_ref, psem.at[1]),
@@ -66,17 +77,6 @@
         a.start()
         b.start()
         loads.append((a, b))
-
-    def signal(sem, x_, y_, z_, c_):
-        pl.semaphore_signal(sem, inc=1, device_id=dev(x_, y_, z_, c_), device_id_type=MESH)
-
-    barrier = pltpu.get_barrier_semaphore()
-    for d in (1, NZ - 1):
-        signal(barrier, x, y, mod(z + d, NZ), c)
-    for d in (1, NY - 1):
-        signal(barrier, x, mod(y + d, NY), z, c)
-    for dx, dc in XC:
-        signal(barrier, mod(x + dx, NX), y, z, mod(c + dc, NC))
 
     for cp in picks:
         cp.wait()
@@ -94,13 +94,20 @@
     source4 = jnp.concatenate([source] * 4, axis=1)
     for j in range(CHUNKS):
         for d in range(8):
-            idsend[j, d] = target4[8 * j + d : 8 * j + d + 1]
+            idsend[d, j] = target4[8 * j + d : 8 * j + d + 1]
     source_t = jnp.transpose(source4.astype(F32)).astype(I32)
     lane128 = lax.broadcasted_iota(I32, (1, 128), 1)
     lane256 = lax.broadcasted_iota(I32, (64, 256), 1)
     sub256 = lax.broadcasted_iota(I32, (256, 128), 0)
     ones = jnp.ones((128, 128), BF16)
 
+    def accumulated(top):
+        rows = []
+        for q in range(32):
+            lanes = slice(128 * q, 128 * (q + 1))
+            rows.append(gv[top : top + 8, lanes].astype(F32) + rv[top : top + 8, lanes])
+        return jnp.concatenate(rows, axis=0)
+
     mine = 2 * x + c
     idcopies = []
     xcopies = []
@@ -110,11 +117,7 @@
         for p in range(4):
             s = 8 * j + 2 * p
             top = 32 * j + 8 * p
-            blocks = []
-            for q in range(32):
-                lanes = slice(128 * q, 128 * (q + 1))
-                blocks.append(gv[top : top + 8, lanes].astype(F32) + rv[top : top + 8, lanes])
-            data = jnp.concatenate(blocks, axis=0)
+            data = accumulated(top)
             ids = jnp.concatenate(
                 [
                     jnp.broadcast_to(source_t[:32, s : s + 1], (32, 256)),
@@ -126,12 +129,6 @@
             got = joined(jnp.dot(pick, halves(data), preferred_element_type=F32))
             xsend[j, 2 * p] = got[:32]
             xsend[j, 2 * p + 1] = got[32:]
-            row = jnp.where(lane128 < 32, source4[s : s + 1], source4[s + 1 : s + 2])
-            hit = jnp.where(jnp.broadcast_to(row, (256, 128)) == sub256, 1.0, 0.0).astype(BF16)
-            mask = jnp.dot(hit, ones, preferred_element_type=F32)
-            kept = jnp.where(mask > 0.5, 0.0, data)
-            for q in range(32):
-                nr_ref[0, 0, top : top + 8, 128 * q : 128 * (q + 1)] = kept[8 * q : 8 * q + 8]
         if j == 0:
             pl.semaphore_wait(barrier, 11)
             for d in (1, NZ - 1):
@@ -141,13 +138,13 @@
             for n, (dx, dc) in enumerate(XC):
                 tx, tc = mod(x + dx, NX), mod(c + dc, NC)
                 cp = pltpu.make_async_remote_copy(
-                    src_ref=idsend.at[:, 2 * tx + tc], dst_ref=idrecv.at[n + 1],
+                    src_ref=idsend.at[2 * tx + tc], dst_ref=idrecv.at[n + 1],
                     send_sem=ids_s.at[n], recv_sem=ids_r.at[n],
                     device_id=dev(tx, y, z, tc), device_id_type=MESH,
                 )
                 cp.start()
                 idcopies.append(cp)
-            idrecv[0] = idsend[:, mine]
+            idrecv[0] = idsend[mine]
         if j == 1:
             pl.semaphore_wait(near1, 4)
             for d in (2, NZ - 2):
@@ -166,6 +163,14 @@
             copies.append(cp)
         xrecv[j, 0] = xsend[j, mine]
         xcopies.append(copies)
+        for p in range(4 * j, 4 * j + 4):
+            s, top = 2 * p, 8 * p
+            row = jnp.where(lane128 < 32, source4[s : s + 1], source4[s + 1 : s + 2])
+            hit = jnp.where(jnp.broadcast_to(row, (256, 128)) == sub256, 1.0, 0.0).astype(BF16)
+            mask = jnp.dot(hit, ones, preferred_element_type=F32)
+            kept = jnp.where(mask > 0.5, 0.0, accumulated(top))
+            for q in range(32):
+                nr_ref[0, 0, top : top + 8, 128 * q : 128 * (q + 1)] = kept[8 * q : 8 * q + 8]
 
     pl.semaphore_wait(near2, 4)
     for d in (3, NZ - 3):
@@ -202,40 +207,53 @@
 
     pl.semaphore_wait(near3, 2)
     zx = lax.rem(z, NX)
+
+    def z_copy(j, h):
+        return pltpu.make_async_remote_copy(
+            src_ref=zsend.at[j, h], dst_ref=zrecv.at[z],
+            send_sem=zs.at[j, h], recv_sem=zr.at[z],
+            device_id=dev(mod(x + h, NX), y, 4 * j + x, c), device_id_type=MESH,
+        )
+
+    second = mod(zx + 1, NX) == x
+    half = mod(x - zx, NX)
+
+    def g_copy(n, dx, dy):
+        return pltpu.make_async_remote_copy(
+            src_ref=fin, dst_ref=gbuf.at[y, half],
+            send_sem=as_.at[n], recv_sem=ar.at[y, half],
+            device_id=dev(mod(x + dx, NX), mod(y + dy, NY), z, c), device_id_type=MESH,
+        )
+
     for j in range(CHUNKS):
         for cp in ycopies[j]:
             cp.wait_recv()
         total = ysend[j, y]
         for n in range(NY - 1):
             total = total + yrecv[j, n]
-        zsend[j] = total
+        zsend[j, 0] = total[:8]
+        zsend[j, 1] = total[8:]
         tz = 4 * j + x
-
-        def same_x(j=j, tz=tz):
-            return pltpu.make_async_remote_copy(
-                src_ref=zsend.at[j], dst_ref=zrecv.at[z],
-                send_sem=zs.at[j], recv_sem=zr.at[z],
-                device_id=dev(x, y, tz, c), device_id_type=MESH,
-            )
+        z_copy(j, 1).start()
 
         @pl.when(tz != z)
-        def _():
-            same_x().start()
+        def _(j=j):
+            z_copy(j, 0).start()
 
         @pl.when(tz == z)
-        def _():
-            zrecv[z] = zsend[j]
-
-    owner = zx == x
+        def _(total=total):
+            zrecv[z] = total[:8]
+
+    owner = jnp.logical_or(zx == x, second)
 
     @pl.when(owner)
     def _():
         for s in range(NZ):
-            @pl.when(z != s)
+            @pl.when(jnp.logical_or(z != s, second))
             def _():
                 pltpu.make_async_remote_copy(
-                    src_ref=zsend.at[0], dst_ref=zrecv.at[s],
-                    send_sem=zs.at[0], recv_sem=zr.at[s],
+                    src_ref=zsend.at[0, 0], dst_ref=zrecv.at[s],
+                    send_sem=zs.at[0, 0], recv_sem=zr.at[s],
                     device_id=dev(x, y, z, 1 - c), device_id_type=MESH,
                 ).wait_recv()
 
@@ -245,12 +263,8 @@
         result = result * (1.0 / 32.0)
         fin[...] = result
         for n, (dx, dy) in enumerate(GS):
-            pltpu.make_async_remote_copy(
-                src_ref=fin, dst_ref=gbuf.at[y],
-                send_sem=as_.at[n], recv_sem=ar.at[y],
-                device_id=dev(mod(x + dx, NX), mod(y + dy, NY), z, c), device_id_type=MESH,
-            ).start()
-        gbuf[y] = result
+            g_copy(n, dx, dy).start()
+        gbuf[y, half] = result
 
     for cp in idcopies:
         cp.wait_send()
@@ -258,35 +272,28 @@
         for cp in copies:
             cp.wait_send()
     for j in range(CHUNKS):
-        tz = 4 * j + x
-
-        @pl.when(tz != z)
-        def _():
-            pltpu.make_async_remote_copy(
-                src_ref=zsend.at[j], dst_ref=zrecv.at[z],
-                send_sem=zs.at[j], recv_sem=zr.at[z],
-                device_id=dev(x, y, tz, c), device_id_type=MESH,
-            ).wait_send()
+        z_copy(j, 1).wait_send()
+
+        @pl.when(4 * j + x != z)
+        def _(j=j):
+            z_copy(j, 0).wait_send()
     for s in range(NY):
-        @pl.when(jnp.logical_or(zx != x, y != s))
-        def _():
-            pltpu.make_async_remote_copy(
-                src_ref=fin, dst_ref=gbuf.at[s],
-                send_sem=as_.at[0], recv_sem=ar.at[s],
-                device_id=dev(x, y, z, 1 - c), device_id_type=MESH,
-            ).wait_recv()
+        for h in range(2):
+            @pl.when(jnp.logical_or(mod(zx + h, NX) != x, y != s))
+            def _(s=s, h=h):
+                pltpu.make_async_remote_copy(
+                    src_ref=fin, dst_ref=gbuf.at[s, h],
+                    send_sem=as_.at[0], recv_sem=ar.at[s, h],
+                    device_id=dev(x, y, z, 1 - c), device_id_type=MESH,
+                ).wait_recv()
 
     @pl.when(owner)
     def _():
         for n, (dx, dy) in enumerate(GS):
-            pltpu.make_async_remote_copy(
-                src_ref=fin, dst_ref=gbuf.at[y],
-                send_sem=as_.at[n], recv_sem=ar.at[y],
-                device_id=dev(mod(x + dx, NX), mod(y + dy, NY), z, c), device_id_type=MESH,
-            ).wait_send()
+            g_copy(n, dx, dy).wait_send()
 
     for p in range(32):
-        upd_ref[0, :, 128 * p : 128 * (p + 1)] = gbuf[p // 4, 4 * (p % 4) : 4 * (p % 4) + 4]
+        upd_ref[0, :, 128 * p : 128 * (p + 1)] = gbuf[p // 4, p // 2 % 2, 4 * (p % 2) : 4 * (p % 2) + 4]
 
 
 def flush(upd_ref, nr_ref, upd_hbm, nr_hbm, sem):
@@ -321,20 +328,20 @@
             pltpu.VMEM((96, 4096), F32),
             pltpu.VMEM((CHUNKS, 8, 32, 128), F32),
             pltpu.VMEM((CHUNKS, 8, 32, 128), F32),
-            pltpu.VMEM((CHUNKS, 8, 1, 128), I32),
+            pltpu.VMEM((8, CHUNKS, 1, 128), I32),
             pltpu.VMEM((8, CHUNKS, 1, 128), I32),
             pltpu.VMEM((CHUNKS, 8, 16, 128), F32),
             pltpu.VMEM((CHUNKS, 7, 16, 128), F32),
-            pltpu.VMEM((CHUNKS, 16, 128), F32),
-            pltpu.VMEM((NZ, 16, 128), F32),
-            pltpu.VMEM((16, 128), F32),
-            pltpu.VMEM((NY, 16, 128), F32),
+            pltpu.VMEM((CHUNKS, 2, 8, 128), F32),
+            pltpu.VMEM((NZ, 8, 128), F32),
+            pltpu.VMEM((8, 128), F32),
+            pltpu.VMEM((NY, 2, 8, 128), F32),
             dma((2,)), dma((CHUNKS,)), dma((CHUNKS,)),
             dma((CHUNKS, 7)), dma((CHUNKS, 7)),
             dma((7,)), dma((7,)),
             dma((CHUNKS, 7)), dma((CHUNKS, 7)),
-            dma((CHUNKS,)), dma((NZ,)),
-            dma((31,)), dma((NY,)),
+            dma((CHUNKS, 2)), dma((NZ,)),
+            dma((31,)), dma((NY, 2)),
             plain, plain, plain,
         ],
         compiler_params=pltpu.CompilerParams(collective_id=0, has_side_effects=True, vmem_limit_bytes=62 << 20),

time: 40.5 us -> 40 us (0.988)
  Pallas kernels: 39.7 us -> 39.2 us
    pallas_call x1, Pallas kernels: 38.5 us -> 38 us  [body(): pl.pallas_call(kernel, name='owner_sums', out_shape=(pltpu.VMEM((1, 4, 40...]
where the time goes in v4:
time: 40 us; the launch traced here: 39.8 us
  Pallas kernels  39.2 us (98%)
  between operations  0.64 us (2%)
    pallas_call x1, Pallas kernels, body(): pl.pallas_call(kernel, name='owner_sums', out_shape=(pltpu.VMEM((1, 4, 40...  38 us
    pallas_call x1, Pallas kernels, body(): pl.pallas_call(flush, name='write_results', out_shape=(jax.ShapeDtypeStru...  1.2 us

profile of v4, /device:TPU:6, one launch (start us, length us, event | category | flops | bytes accessed | tf_op | source)
XLA Modules:
  0.0 39.8 jit_solution(7209089427589360539)
XLA Ops:
  0.6 38.0 %owner_sums.1 = (f32[1,4,4096]{2,1,0:T(4,128)S(1)}, f32[1,1,96,4096]{3,2,1,0:T(8,128)S(1)}) custom-call(bf16[1,1,96,4096]{3,2,1,0:T(8,128)(2,1)} %g_hbm.1, f32[1,1,96,4096]{3,2,1,0:T(8,128)} %r_hbm.1, s32[1,1,24,32]{3,2,1,0:T(8,128)} %sel_hbm.1, s32[1,1,24]{2,1,0:T(1,128)} %cnt_hbm.1), custom_call_target="tpu_custom_call" | custom-call | tf_op jit(solution)/shard_map/owner_sums/pallas_call | solution.py:315
  38.6 1.2 %write_results.1 = (f32[1,4,4096]{2,1,0:T(4,128)}, f32[1,1,96,4096]{3,2,1,0:T(8,128)}) custom-call(f32[1,4,4096]{2,1,0:T(4,128)S(1)} %get-tuple-element.4.upd_ref, f32[1,1,96,4096]{3,2,1,0:T(8,128)S(1)} %get-tuple-element.5.nr_ref), custom_call_target="tpu_custom_call" | custom-call | tf_op jit(solution)/shard_map/write_results/pallas_call | solution.py:349
